TPU v7x, 128 devices: a whole 4x4x4 slice. The times are simulated.
128 devices in a mesh: dp: 8 (over y_lo, x), tensor: 16 (over z, y_hi, core).
Axes of the slice: x: 4, y: 4 (y_hi: 2, y_lo: 2; y = y_hi * 2 + y_lo), z: 4, core: 2. Of those that a mesh axis runs over, the one named last changes fastest.
Arguments:
- tokens: bfloat16 [8192, 2048], P(('dp', 'tensor')), may hold values from -12 to 12
- targets: bfloat16 [8192, 2048], P(('dp', 'tensor')), may hold values from -6 to 6
- learner_gain: float32 [2048], replicated, may hold values from 0.1 to 1.9
- learner_gate: bfloat16 [2048, 8192], P(None, 'tensor'), may hold values from -0.125 to 0.125
- learner_up: bfloat16 [2048, 8192], P(None, 'tensor'), may hold values from -0.125 to 0.125
- learner_down: bfloat16 [8192, 2048], P('tensor'), may hold values from -0.0625 to 0.0625
- frozen_gain: float32 [2048], replicated, may hold values from 0.1 to 1.9
- frozen_gate: bfloat16 [2048, 8192], P(None, 'tensor'), may hold values from -0.125 to 0.125
- frozen_up: bfloat16 [2048, 8192], P(None, 'tensor'), may hold values from -0.125 to 0.125
- frozen_down: bfloat16 [8192, 2048], P('tensor'), may hold values from -0.0625 to 0.0625
Outputs:
- scores: float32 [8192], P(('dp', 'tensor'))
- grad_tokens: bfloat16 [8192, 2048], P(('dp', 'tensor'))
- grad_gain: float32 [2048], replicated
- grad_gate: float32 [2048, 8192], P('dp', 'tensor')
- grad_up: float32 [2048, 8192], P('dp', 'tensor')
- grad_down: float32 [8192, 2048], P('tensor', 'dp')
All inputs are finite; a program needn't handle non-finite values.
Results may differ from a plain program's by a relative error of at most 0.0096.
Values may be sent and summed in bfloat16 or wider, within the bound.
A program may use at most 128 MiB of HBM per device.

v0:
```python
import math
import jax
import jax.numpy as jnp
from jax import lax
from jax.sharding import PartitionSpec as P


def in_one_piece(arrays, axis, dim, along):
    both = jnp.concatenate(arrays, axis=along)
    out, at, gathered = (lax.all_gather(both, axis, axis=dim, tiled=True), 0, [])
    for a in arrays:
        gathered.append(lax.slice_in_dim(out, at, at + a.shape[along], axis=along))
        at += a.shape[along]
    return tuple(gathered)


def split_up(value, dim, size):
    shape = value.shape
    blocks = value.reshape(*shape[:dim], size, shape[dim] // size, *shape[dim + 1 :])
    return jnp.moveaxis(blocks, dim, 0)


def sum_at_owner(value, axis, dim):
    blocks = split_up(value, dim, lax.axis_size(axis))
    arrived = lax.all_to_all(blocks, axis, split_axis=0, concat_axis=0, tiled=True)
    return arrived.astype(jnp.float32).sum(axis=0)


def sent_together(arrays, axis, dim, along):
    widths = [a.shape[along] for a in arrays]
    both = jnp.concatenate(arrays, axis=along)
    out = sum_at_owner(both, axis, dim)
    return tuple(jnp.split(out, [sum(widths[:k]) for k in range(1, len(widths))], axis=along))


def project_up(normed, w_gate, w_up, w_down):
    gate_pre = jnp.dot(normed, w_gate, preferred_element_type=jnp.float32)
    up_pre = jnp.dot(normed, w_up, preferred_element_type=jnp.float32)
    hidden = (jax.nn.silu(gate_pre) * up_pre).astype(jnp.bfloat16)
    partial_out = jnp.dot(hidden, w_down, preferred_element_type=jnp.float32)
    return (gate_pre, up_pre, hidden, partial_out)


def local(
    tokens,
    targets,
    learner_gain,
    learner_gate,
    learner_up,
    learner_down,
    frozen_gain,
    frozen_gate,
    frozen_up,
    frozen_down,
):
    xfloat = tokens.astype(jnp.float32)
    inv_rms = lax.rsqrt(jnp.mean(xfloat * xfloat, axis=-1, keepdims=True) + 1e-05)
    normed = (xfloat * inv_rms * learner_gain).astype(jnp.bfloat16)
    frozen_normed = (xfloat * inv_rms * frozen_gain).astype(jnp.bfloat16)
    normed_all, frozen_all = in_one_piece((normed, frozen_normed), "tensor", 0, 1)
    gate_pre, up_pre, hidden, partial_learned = project_up(
        normed_all, learner_gate, learner_up, learner_down
    )
    frozen_partial = project_up(frozen_all, frozen_gate, frozen_up, frozen_down)[3]
    learned, frozen_out = sent_together(
        (partial_learned.astype(jnp.bfloat16), frozen_partial.astype(jnp.bfloat16)), "tensor", 0, 1
    )
    goal = targets.astype(jnp.float32)
    root = math.sqrt(tokens.shape[1])
    miss = learned - goal
    frozen_miss = frozen_out - goal
    learner_loss = 0.5 * jnp.sum(miss * miss, axis=-1) / root
    frozen_loss = 0.5 * jnp.sum(frozen_miss * frozen_miss, axis=-1) / root
    scores = learner_loss - frozen_loss
    weight = jax.nn.sigmoid(scores)
    out_grad = (weight[:, None] * miss / root).astype(jnp.bfloat16)
    grads_all = lax.all_gather(out_grad, "tensor", axis=0, tiled=True)
    hidden_grad = jnp.dot(grads_all, learner_down.T, preferred_element_type=jnp.float32)
    sigma = jax.nn.sigmoid(gate_pre)
    gate_grad = (hidden_grad * up_pre * sigma * (1.0 + gate_pre * (1.0 - sigma))).astype(
        jnp.bfloat16
    )
    up_grad = (hidden_grad * gate_pre * sigma).astype(jnp.bfloat16)
    partial_normed = jnp.dot(
        gate_grad, learner_gate.T, preferred_element_type=jnp.float32
    ) + jnp.dot(up_grad, learner_up.T, preferred_element_type=jnp.float32)
    normed_grad = sum_at_owner(partial_normed.astype(jnp.bfloat16), "tensor", 0)
    gain_term = jnp.sum(normed_grad * xfloat * inv_rms, axis=0)
    grad_gain = lax.psum(gain_term, ("dp", "tensor"))
    scaled = learner_gain * normed_grad
    cubed = inv_rms * inv_rms * inv_rms
    grad_tokens = (
        inv_rms * scaled - xfloat * cubed * jnp.mean(scaled * xfloat, axis=-1, keepdims=True)
    ).astype(jnp.bfloat16)
    gate_term = jnp.einsum("td,tf->df", normed_all, gate_grad, preferred_element_type=jnp.float32)
    up_term = jnp.einsum("td,tf->df", normed_all, up_grad, preferred_element_type=jnp.float32)
    down_term = jnp.einsum("td,tf->df", grads_all, hidden, preferred_element_type=jnp.float32)
    grad_gate, grad_up, down_shard = sent_together(
        (
            gate_term.astype(jnp.bfloat16),
            up_term.astype(jnp.bfloat16),
            down_term.astype(jnp.bfloat16),
        ),
        "dp",
        0,
        1,
    )
    grad_down = down_shard.T
    return (scores, grad_tokens, grad_gain, grad_gate, grad_up, grad_down)


def solution(mesh):
    placed = (
        P(("dp", "tensor"), None),
        P(("dp", "tensor"), None),
        P(),
        P(None, "tensor"),
        P(None, "tensor"),
        P("tensor", None),
        P(),
        P(None, "tensor"),
        P(None, "tensor"),
        P("tensor", None),
    )
    return jax.shard_map(
        local,
        mesh=mesh,
        in_specs=placed,
        out_specs=(
            P(("dp", "tensor")),
            P(("dp", "tensor"), None),
            P(),
            P("dp", "tensor"),
            P("dp", "tensor"),
            P("tensor", "dp"),
        ),
        check_vma=False,
    )
```

profile of v0, /device:TPU:1, one launch (start us, length us, event | category | flops | bytes accessed | tf_op | source)
XLA Modules:
  0.0 515.8 jit_solution(17087560783303499383)
XLA Ops:
  7.2 1.2 fusion.21
  8.5 1.1 fusion.17
  9.6 0.8 pad_maximum_fusion.2
  10.5 77.0 %all-gather.3.cloned.1.call-done = bf16[1024,4096]{1,0:T(8,128)(2,1)} async-done(((bf16[64,4096]{1,0:T(8,128)(2,1)}), bf16[1024,4096]{1,0:T(8,128)(2,1)}) %all-gather.3.cloned.1.call-update) | async-done | bytes 8388624 | tf_op jit(solution)/shard_map/all_gather | solution.py:10
  87.5 5.3 %fusion.8 = f32[1024,512]{1,0:T(8,128)S(1)} fusion(bf16[2048,512]{1,0:T(8,128)(2,1)} %param.13, bf16[1024,4096]{1,0:T(8,128)(2,1)} %all-gather.3.cloned.1.call-done), kind=kOutput, calls=%fused_computation.20 | convolution fusion | flops 2147483648 | bytes 8388608 | tf_op jit(solution)/shard_map/dot_general | solution.py:37
  93.4 3.8 multiply_convert_fusion.3
  97.2 4.3 convolution_convert_fusion.1
  101.5 3.7 fusion.2
  105.2 10.6 %convolution_convert_fusion = bf16[1024,2048]{1,0:T(8,128)(2,1)} fusion(bf16[512,2048]{1,0:T(8,128)(2,1)} %param.19, f32[1024,512]{1,0:T(8,128)} %fusion.2, bf16[2048,512]{1,0:T(8,128)(2,1)} %param.18, bf16[1024,4096]{1,0:T(8,128)(2,1)} %all-gather.3.cloned.1.call-done), kind=kOutput, calls=%fused_computation.7 | convolution fusion | flops 4300210176 | bytes 14680064 | tf_op jit(solution)/shard_map/dot_general | solution.py:40
  115.8 7.8 %pad_maximum_fusion = bf16[1024,4096]{1,0:T(8,128)(2,1)} fusion(bf16[1024,2048]{1,0:T(8,128)(2,1)} %convolution_convert_fusion, bf16[1024,2048]{1,0:T(8,128)(2,1)} %convolution_convert_fusion.1), kind=kLoop, calls=%fused_computation.2 | loop fusion | flops 16777216 | bytes 16777216 | tf_op jit(solution)/shard_map/concatenate | solution.py:31
  123.6 99.4 %all_to_all.15 = bf16[16,64,4096]{2,1,0:T(8,128)(2,1)S(1)} all-to-all(bf16[16,64,4096]{2,1,0:T(8,128)(2,1)} %bitcast.25), channel_id=1, replica_groups=mesh['dp'=8,'tensor'=16] {'tensor'}, dimensions={0} | all-to-all | bytes 16777216 | tf_op jit(solution)/shard_map/all_to_all | solution.py:25
  223.0 1.6 convert_reduce_fusion
  225.3 0.8 multiply_convert_fusion.4
  226.2 52.8 %all-gather.5.cloned.1.call-done = bf16[1024,2048]{1,0:T(8,128)(2,1)} async-done(((bf16[64,2048]{1,0:T(8,128)(2,1)}), bf16[1024,2048]{1,0:T(8,128)(2,1)}) %all-gather.5.cloned.1.call-update) | async-done | bytes 4194320 | tf_op jit(solution)/shard_map/all_gather | solution.py:77
  279.0 6.5 %multiply_convert_fusion = (bf16[1024,512]{1,0:T(8,128)(2,1)S(1)}, bf16[1024,512]{1,0:T(8,128)(2,1)S(1)}) fusion(f32[1024,512]{1,0:T(8,128)} %copy-done.13, f32[1024,512]{1,0:T(8,128)} %get-tuple-element.34, bf16[1024,2048]{1,0:T(8,128)(2,1)} %all-gather.5.cloned.1.call-done, bf16[512,2048]{1,0:T(8,128)(2,1)S(1)} %copy-done), kind=kOutput, calls=%fused_computation.22 | convolution fusion | flops 2154299392 | bytes 12582912 | tf_op jit(solution)/shard_map/dot_general | solution.py:78
  285.6 2.4 fusion.29
  288.0 4.3 add_convert_fusion
  292.3 4.7 all-to-all-start.1
  297.0 5.0 convolution_convert_fusion.2
  302.0 4.7 convolution_convert_fusion.3
  306.8 2.4 convolution_convert_fusion.4
  309.2 9.6 %pad_maximum_fusion.1 = bf16[2048,1536]{0,1:T(8,128)(2,1)S(1)} fusion(bf16[2048,512]{0,1:T(8,128)(2,1)S(1)} %convolution_convert_fusion.2, bf16[2048,512]{0,1:T(8,128)(2,1)S(1)} %convolution_convert_fusion.3, bf16[2048,512]{0,1:T(8,128)(2,1)S(1)} %convolution_convert_fusion.4), kind=kLoop, calls=%fused_computation.6 | loop fusion | flops 18874368 | bytes 12582912 | tf_op jit(solution)/shard_map/concatenate | solution.py:31
  318.8 3.1 copy.23
  321.9 25.9 %all-to-all-done.1 = bf16[16,64,2048]{2,1,0:T(8,128)(2,1)} async-done(((bf16[16,64,2048]{2,1,0:T(8,128)(2,1)}), bf16[16,64,2048]{2,1,0:T(8,128)(2,1)}, u32[]{:S(2)}, u32[]{:S(2)}) %all-to-all-start.1) | async-done | bytes 4194336 | tf_op jit(solution)/shard_map/all_to_all | solution.py:25
  347.8 5.0 all-to-all-start.2
  352.9 3.0 convert_reduce_fusion.2
  356.1 145.1 %psum.7 = f32[2048]{0:T(1024)} all-reduce(f32[2048]{0:T(1024)S(1)} %get-tuple-element.20), channel_id=1, replica_groups=mesh['dp'=8,'tensor'=16] {'dp','tensor'}, use_global_device_ids=true, to_apply=%region_7.8 | all-reduce | flops 2048 | bytes 16384 | tf_op jit(solution)/shard_map/psum | solution.py:89
  501.2 0.9 fusion.24
  502.2 3.9 convert_reduce_fusion.1
  506.1 0.9 slice_bitcast_fusion
  507.0 1.0 copy.20
  508.0 1.0 copy.19
  (43 shorter events, 1.6 us)
Async XLA Ops:
  7.2 90.0 %copy-start = (bf16[512,2048]{1,0:T(8,128)(2,1)S(1)}, bf16[512,2048]{1,0:T(8,128)(2,1)}, u32[]{:S(2)}) copy-start(bf16[512,2048]{1,0:T(8,128)(2,1)} %param.15) | copy-start | bytes 6291460
  7.2 80.3 %all-gather.3.cloned.1.call-start = ((), (), s32[]{:S(2)}) async-start(), calls=%async_computation.3 | async-start | bytes 8912896 | tf_op jit(solution)/shard_map/all_gather | solution.py:10
  10.5 268.5 %all-gather.5.cloned.1.call-start = ((), (), s32[]{:S(2)}) async-start(), calls=%async_computation.4 | async-start | bytes 4456448 | tf_op jit(solution)/shard_map/all_gather | solution.py:77
  87.5 5.3 %copy-start.5 = (bf16[1024,4096]{1,0:T(8,128)(2,1)S(1)}, bf16[1024,4096]{1,0:T(8,128)(2,1)}, u32[]{:S(2)}) copy-start(bf16[1024,4096]{1,0:T(8,128)(2,1)} %all-gather.3.cloned.1.call-done) | copy-start | bytes 25165828
  87.5 5.8 %copy-start.8 = (bf16[2048,512]{1,0:T(8,128)(2,1)S(1)}, bf16[2048,512]{1,0:T(8,128)(2,1)}, u32[]{:S(2)}) copy-start(bf16[2048,512]{1,0:T(8,128)(2,1)} %param.14) | copy-start | bytes 6291460
  93.4 3.8 copy-start.13
  97.2 4.3 copy-start.12
  97.2 4.3 copy-start.6
  223.0 1.6 copy-start.3
  279.0 6.6 %copy-start.7 = (bf16[2048,512]{1,0:T(8,128)(2,1)S(1)}, bf16[2048,512]{1,0:T(8,128)(2,1)}, u32[]{:S(2)}) copy-start(bf16[2048,512]{1,0:T(8,128)(2,1)} %param.13) | copy-start | bytes 6291460
  285.5 2.4 copy-start.10
  285.5 2.4 copy-start.9
  292.3 55.5 %all-to-all-start.1 = ((bf16[16,64,2048]{2,1,0:T(8,128)(2,1)}), bf16[16,64,2048]{2,1,0:T(8,128)(2,1)}, u32[]{:S(2)}, u32[]{:S(2)}) async-start(bf16[16,64,2048]{2,1,0:T(8,128)(2,1)} %bitcast.28), calls=%async_computation.1 | async-start | bytes 8388608 | tf_op jit(solution)/shard_map/all_to_all | solution.py:25
  296.9 9.8 %slice-start = ((s8[8388608]{0:T(1024)(128)(4,1)}), s8[4194304]{0:T(1024)(128)(4,1)S(1)}, s32[]{:S(2)}) async-start(s8[8388608]{0:T(1024)(128)(4,1)} %bitcast.29), calls=%async_computation.5 | async-start | bytes 8388608
  302.0 4.8 slice-start.1
  302.0 4.8 copy-start.11
  347.8 154.3 %all-to-all-start.2 = ((bf16[8,256,1536]{1,2,0:T(8,128)(2,1)}), bf16[8,256,1536]{1,2,0:T(8,128)(2,1)}, u32[]{:S(2)}, u32[]{:S(2)}) async-start(bf16[8,256,1536]{1,2,0:T(8,128)(2,1)} %bitcast.26), calls=%async_computation.2 | async-start | bytes 12582912 | tf_op jit(solution)/shard_map/all_to_all | solution.py:25
  352.8 3.1 copy-start.2
  352.8 3.1 copy-start.4
  502.2 6.8 %copy-start.1 = (bf16[512,2048]{1,0:T(8,128)(2,1)S(1)}, bf16[512,2048]{1,0:T(8,128)(2,1)}, u32[]{:S(2)}) copy-start(bf16[512,2048]{1,0:T(8,128)(2,1)} %param.15) | copy-start | bytes 6291460
Sparse Core Ops, SparseCore 0:
  11.0 76.4 all-gather.2
  226.3 52.6 all-gather.4
where the time goes:
time: 516 us
  blocking collectives  245 us (47%)
  waiting for transfers between devices  156 us (30%)
  matrix products  53.1 us (10%)
  other arithmetic  31.9 us (6%)
  between operations  14.3 us (3%)
  starting transfers between devices  9.77 us (2%)
  local copies, waits for them, and re-layouts  6.52 us (1%)
    psum x1, blocking collectives, local(): grad_gain = lax.psum(gain_term, ('dp', 'tensor'))  145 us
    all_to_all x1, blocking collectives, sum_at_owner(): lax.all_to_all(blocks, axis, split_axis=0, concat_axis=0, tiled=True)  99.4 us
    all_gather x1, waiting for transfers between devices, in_one_piece(): lax.all_gather(both, axis, axis=dim, tiled=True)  77 us
    all_gather x1, waiting for transfers between devices, local(): grads_all = lax.all_gather(out_grad, 'tensor', axis=0, tiled=True)  52.8 us
    all_to_all x2, waiting for transfers between devices, sum_at_owner(): lax.all_to_all(blocks, axis, split_axis=0, concat_axis=0, tiled=True)  25.9 us
    concatenate x2, other arithmetic, sent_together(): both = jnp.concatenate(arrays, axis=along)  17.4 us
    dot_general x2, matrix products, project_up(): partial_out = jnp.dot(hidden, w_down, preferred_element_type=jnp.float32)  14.9 us
  transfers between devices with their start and end apart: 4, of which 3 were waited for; matrix products, arithmetic and copies ran while one was open for 6% of the time, Pallas kernels for 0%

commit v1 on v0

--- a/solution.py
+++ b/solution.py
@@ -3,6 +3,7 @@
 import jax.numpy as jnp
 from jax import lax
 from jax.sharding import PartitionSpec as P
+from jax.lax import psum
 
 
 def in_one_piece(arrays, axis, dim, along):
@@ -86,7 +87,7 @@
     ) + jnp.dot(up_grad, learner_up.T, preferred_element_type=jnp.float32)
     normed_grad = sum_at_owner(partial_normed.astype(jnp.bfloat16), "tensor", 0)
     gain_term = jnp.sum(normed_grad * xfloat * inv_rms, axis=0)
-    grad_gain = lax.psum(gain_term, ("dp", "tensor"))
+    grad_gain = psum(psum(gain_term, "tensor"), "dp")
     scaled = learner_gain * normed_grad
     cubed = inv_rms * inv_rms * inv_rms
     grad_tokens = (

time: 516 us -> 484 us (0.938); the launches traced: 516 us -> 476 us
  blocking collectives: 245 us -> 205 us
    psum x1 -> x2, blocking collectives: 145 us -> 105 us  [local(): grad_gain = psum(psum(gain_term, 'tensor'), 'dp')]
where the time goes in v1:
time: 484 us; the launch traced here: 476 us
  blocking collectives  205 us (42%)
  waiting for transfers between devices  156 us (32%)
  matrix products  53.1 us (11%)
  other arithmetic  31.9 us (7%)
  between operations  14.3 us (3%)
  starting transfers between devices  9.52 us (2%)
  local copies, waits for them, and re-layouts  6.52 us (1%)
    psum x2, blocking collectives, local(): grad_gain = psum(psum(gain_term, 'tensor'), 'dp')  105 us
    all_to_all x1, blocking collectives, sum_at_owner(): lax.all_to_all(blocks, axis, split_axis=0, concat_axis=0, tiled=True)  99.4 us
    all_gather x1, waiting for transfers between devices, in_one_piece(): lax.all_gather(both, axis, axis=dim, tiled=True)  77 us
    all_gather x1, waiting for transfers between devices, local(): grads_all = lax.all_gather(out_grad, 'tensor', axis=0, tiled=True)  52.8 us
    all_to_all x2, waiting for transfers between devices, sum_at_owner(): lax.all_to_all(blocks, axis, split_axis=0, concat_axis=0, tiled=True)  25.9 us
    concatenate x2, other arithmetic, sent_together(): both = jnp.concatenate(arrays, axis=along)  17.4 us
    dot_general x2, matrix products, project_up(): partial_out = jnp.dot(hidden, w_down, preferred_element_type=jnp.float32)  14.9 us
  transfers between devices with their start and end apart: 4, of which 3 were waited for; matrix products, arithmetic and copies ran while one was open for 6% of the time, Pallas kernels for 0%

profile of v1, /device:TPU:1, one launch (start us, length us, event | category | flops | bytes accessed | tf_op | source)
XLA Modules:
  0.0 475.6 jit_solution(14510077146409072441)
XLA Ops:
  7.2 1.2 fusion.21
  8.5 1.1 fusion.17
  9.6 0.8 pad_maximum_fusion.2
  10.5 77.0 %all-gather.3.cloned.1.call-done = bf16[1024,4096]{1,0:T(8,128)(2,1)} async-done(((bf16[64,4096]{1,0:T(8,128)(2,1)}), bf16[1024,4096]{1,0:T(8,128)(2,1)}) %all-gather.3.cloned.1.call-update) | async-done | bytes 8388624 | tf_op jit(solution)/shard_map/all_gather | solution.py:11
  87.5 5.3 %fusion.8 = f32[1024,512]{1,0:T(8,128)S(1)} fusion(bf16[2048,512]{1,0:T(8,128)(2,1)} %param.13, bf16[1024,4096]{1,0:T(8,128)(2,1)} %all-gather.3.cloned.1.call-done), kind=kOutput, calls=%fused_computation.20 | convolution fusion | flops 2147483648 | bytes 8388608 | tf_op jit(solution)/shard_map/dot_general | solution.py:38
  93.4 3.8 multiply_convert_fusion.3
  97.2 4.3 convolution_convert_fusion.1
  101.5 3.7 fusion.2
  105.2 10.6 %convolution_convert_fusion = bf16[1024,2048]{1,0:T(8,128)(2,1)} fusion(bf16[512,2048]{1,0:T(8,128)(2,1)} %param.19, f32[1024,512]{1,0:T(8,128)} %fusion.2, bf16[2048,512]{1,0:T(8,128)(2,1)} %param.18, bf16[1024,4096]{1,0:T(8,128)(2,1)} %all-gather.3.cloned.1.call-done), kind=kOutput, calls=%fused_computation.7 | convolution fusion | flops 4300210176 | bytes 14680064 | tf_op jit(solution)/shard_map/dot_general | solution.py:41
  115.8 7.8 %pad_maximum_fusion = bf16[1024,4096]{1,0:T(8,128)(2,1)} fusion(bf16[1024,2048]{1,0:T(8,128)(2,1)} %convolution_convert_fusion, bf16[1024,2048]{1,0:T(8,128)(2,1)} %convolution_convert_fusion.1), kind=kLoop, calls=%fused_computation.2 | loop fusion | flops 16777216 | bytes 16777216 | tf_op jit(solution)/shard_map/concatenate | solution.py:32
  123.6 99.4 %all_to_all.15 = bf16[16,64,4096]{2,1,0:T(8,128)(2,1)S(1)} all-to-all(bf16[16,64,4096]{2,1,0:T(8,128)(2,1)} %bitcast.25), channel_id=1, replica_groups=mesh['dp'=8,'tensor'=16] {'tensor'}, dimensions={0} | all-to-all | bytes 16777216 | tf_op jit(solution)/shard_map/all_to_all | solution.py:26
  223.0 1.6 convert_reduce_fusion
  226.2 52.8 %all-gather.5.cloned.1.call-done = bf16[1024,2048]{1,0:T(8,128)(2,1)} async-done(((bf16[64,2048]{1,0:T(8,128)(2,1)}), bf16[1024,2048]{1,0:T(8,128)(2,1)}) %all-gather.5.cloned.1.call-update) | async-done | bytes 4194320 | tf_op jit(solution)/shard_map/all_gather | solution.py:78
  279.0 6.5 %multiply_convert_fusion = (bf16[1024,512]{1,0:T(8,128)(2,1)S(1)}, bf16[1024,512]{1,0:T(8,128)(2,1)S(1)}) fusion(f32[1024,512]{1,0:T(8,128)} %copy-done.13, f32[1024,512]{1,0:T(8,128)} %get-tuple-element.34, bf16[1024,2048]{1,0:T(8,128)(2,1)} %all-gather.5.cloned.1.call-done, bf16[512,2048]{1,0:T(8,128)(2,1)S(1)} %copy-done), kind=kOutput, calls=%fused_computation.22 | convolution fusion | flops 2154299392 | bytes 12582912 | tf_op jit(solution)/shard_map/dot_general | solution.py:79
  285.5 2.4 fusion.29
  287.9 4.3 add_convert_fusion
  292.2 4.7 all-to-all-start.1
  297.0 5.0 %convolution_convert_fusion.2 = bf16[2048,512]{0,1:T(8,128)(2,1)S(1)} fusion(bf16[1024,2048]{1,0:T(8,128)(2,1)} %all-gather.5.cloned.1.call-done, bf16[1024,512]{1,0:T(8,128)(2,1)} %copy-done.12), kind=kOutput, calls=%fused_computation.13 | convolution fusion | flops 2148532224 | bytes 7340032 | tf_op jit(solution)/shard_map/td,tf->df/dot_general | solution.py:98
  302.0 4.7 convolution_convert_fusion.3
  306.8 2.4 convolution_convert_fusion.4
  309.2 9.6 %pad_maximum_fusion.1 = bf16[2048,1536]{0,1:T(8,128)(2,1)S(1)} fusion(bf16[2048,512]{0,1:T(8,128)(2,1)S(1)} %convolution_convert_fusion.2, bf16[2048,512]{0,1:T(8,128)(2,1)S(1)} %convolution_convert_fusion.3, bf16[2048,512]{0,1:T(8,128)(2,1)S(1)} %convolution_convert_fusion.4), kind=kLoop, calls=%fused_computation.6 | loop fusion | flops 18874368 | bytes 12582912 | tf_op jit(solution)/shard_map/concatenate | solution.py:32
  318.8 3.1 copy.23
  321.9 25.9 %all-to-all-done.1 = bf16[16,64,2048]{2,1,0:T(8,128)(2,1)} async-done(((bf16[16,64,2048]{2,1,0:T(8,128)(2,1)}), bf16[16,64,2048]{2,1,0:T(8,128)(2,1)}, u32[]{:S(2)}, u32[]{:S(2)}) %all-to-all-start.1) | async-done | bytes 4194336 | tf_op jit(solution)/shard_map/all_to_all | solution.py:26
  347.8 4.8 all-to-all-start.2
  352.6 3.0 convert_reduce_fusion.2
  355.8 82.0 %psum.14 = f32[2048]{0:T(1024)S(1)} all-reduce(f32[2048]{0:T(1024)S(1)} %get-tuple-element.20), channel_id=1, replica_groups=mesh['dp'=8,'tensor'=16] {'tensor'}, use_global_device_ids=true, to_apply=%region_7.8 | all-reduce | flops 2048 | bytes 16384 | tf_op jit(solution)/shard_map/psum | solution.py:90
  437.8 23.2 %psum.15 = f32[2048]{0:T(1024)} all-reduce(f32[2048]{0:T(1024)S(1)} %psum.14), channel_id=1, replica_groups=mesh['dp'=8,'tensor'=16] {'dp'}, use_global_device_ids=true, to_apply=%region_8.9 | all-reduce | flops 2048 | bytes 16384 | tf_op jit(solution)/shard_map/psum | solution.py:90
  461.0 0.9 fusion.24
  461.9 3.9 convert_reduce_fusion.1
  465.9 0.9 slice_bitcast_fusion
  466.8 1.0 copy.20
  467.8 1.0 copy.19
  (44 shorter events, 2.4 us)
Async XLA Ops:
  7.2 90.0 %copy-start = (bf16[512,2048]{1,0:T(8,128)(2,1)S(1)}, bf16[512,2048]{1,0:T(8,128)(2,1)}, u32[]{:S(2)}) copy-start(bf16[512,2048]{1,0:T(8,128)(2,1)} %param.15) | copy-start | bytes 6291460
  7.2 80.3 %all-gather.3.cloned.1.call-start = ((), (), s32[]{:S(2)}) async-start(), calls=%async_computation.3 | async-start | bytes 8912896 | tf_op jit(solution)/shard_map/all_gather | solution.py:11
  10.5 268.5 %all-gather.5.cloned.1.call-start = ((), (), s32[]{:S(2)}) async-start(), calls=%async_computation.4 | async-start | bytes 4456448 | tf_op jit(solution)/shard_map/all_gather | solution.py:78
  87.5 5.3 %copy-start.5 = (bf16[1024,4096]{1,0:T(8,128)(2,1)S(1)}, bf16[1024,4096]{1,0:T(8,128)(2,1)}, u32[]{:S(2)}) copy-start(bf16[1024,4096]{1,0:T(8,128)(2,1)} %all-gather.3.cloned.1.call-done) | copy-start | bytes 25165828
  87.5 5.8 %copy-start.8 = (bf16[2048,512]{1,0:T(8,128)(2,1)S(1)}, bf16[2048,512]{1,0:T(8,128)(2,1)}, u32[]{:S(2)}) copy-start(bf16[2048,512]{1,0:T(8,128)(2,1)} %param.14) | copy-start | bytes 6291460
  93.4 3.8 copy-start.13
  97.2 4.3 copy-start.12
  97.2 4.3 copy-start.6
  223.0 1.6 copy-start.3
  279.0 6.6 %copy-start.7 = (bf16[2048,512]{1,0:T(8,128)(2,1)S(1)}, bf16[2048,512]{1,0:T(8,128)(2,1)}, u32[]{:S(2)}) copy-start(bf16[2048,512]{1,0:T(8,128)(2,1)} %param.13) | copy-start | bytes 6291460
  285.5 2.4 copy-start.10
  285.5 2.4 copy-start.9
  292.2 55.6 %all-to-all-start.1 = ((bf16[16,64,2048]{2,1,0:T(8,128)(2,1)}), bf16[16,64,2048]{2,1,0:T(8,128)(2,1)}, u32[]{:S(2)}, u32[]{:S(2)}) async-start(bf16[16,64,2048]{2,1,0:T(8,128)(2,1)} %bitcast.28), calls=%async_computation.1 | async-start | bytes 8388608 | tf_op jit(solution)/shard_map/all_to_all | solution.py:26
  296.9 9.8 %slice-start = ((s8[8388608]{0:T(1024)(128)(4,1)}), s8[4194304]{0:T(1024)(128)(4,1)S(1)}, s32[]{:S(2)}) async-start(s8[8388608]{0:T(1024)(128)(4,1)} %bitcast.29), calls=%async_computation.5 | async-start | bytes 8388608
  302.0 4.8 %slice-start.1 = ((s8[8388608]{0:T(1024)(128)(4,1)}), s8[4194304]{0:T(1024)(128)(4,1)S(1)}, s32[]{:S(2)}) async-start(s8[8388608]{0:T(1024)(128)(4,1)} %bitcast.29), calls=%async_computation.6 | async-start | bytes 8388608
  302.0 4.8 %copy-start.11 = (bf16[1024,512]{1,0:T(8,128)(2,1)S(1)}, bf16[1024,512]{1,0:T(8,128)(2,1)}, u32[]{:S(2)}) copy-start(bf16[1024,512]{1,0:T(8,128)(2,1)} %copy-done.10) | copy-start | bytes 3145732
  347.8 114.1 %all-to-all-start.2 = ((bf16[8,256,1536]{1,2,0:T(8,128)(2,1)}), bf16[8,256,1536]{1,2,0:T(8,128)(2,1)}, u32[]{:S(2)}, u32[]{:S(2)}) async-start(bf16[8,256,1536]{1,2,0:T(8,128)(2,1)} %bitcast.26), calls=%async_computation.2 | async-start | bytes 12582912 | tf_op jit(solution)/shard_map/all_to_all | solution.py:26
  352.6 3.1 copy-start.2
  352.6 3.1 copy-start.4
  461.9 6.8 %copy-start.1 = (bf16[512,2048]{1,0:T(8,128)(2,1)S(1)}, bf16[512,2048]{1,0:T(8,128)(2,1)}, u32[]{:S(2)}) copy-start(bf16[512,2048]{1,0:T(8,128)(2,1)} %param.15) | copy-start | bytes 6291460
Sparse Core Ops, SparseCore 0:
  11.0 76.4 all-gather.2
  226.3 52.6 all-gather.4
